TPU v7x, 32 devices: a whole 2x2x4 slice. The times are simulated.
32 devices in a mesh: gx: 4 (over y, x), gy: 4 (over z), gz: 2 (over core).
Axes of the slice: x: 2, y: 2, z: 4, core: 2. Of those that a mesh axis runs over, the one named last changes fastest.
Arguments:
- material: int32 [128, 256, 256], P('gx', 'gy', 'gz'), may hold values from 0 to 7
- eps_table: float32 [8], replicated, may hold values from 1 to 13
- grading: bfloat16 [128, 256, 256], P('gx', 'gy', 'gz'), may hold values from 0.25 to 1.75
Outputs:
- smoothed: bfloat16 [6, 128, 256, 256], P(None, 'gx', 'gy', 'gz')
All inputs are finite; a program needn't handle non-finite values.
Results may differ from a plain program's by a relative error of at most 0.001.
Values sent between devices are 32-bit elements; how exact they have to be, the bound alone decides.
A program may use at most 64 MiB of HBM per device.

v0:
```python
import jax
import jax.numpy as jnp
from jax import lax
from jax.sharding import PartitionSpec as P


def padded_2(block, sides, width):
    for axis, dim in sides:
        count = lax.axis_size(axis)
        forward = [(i, i + 1) for i in range(count - 1)]
        forward.append((count - 1, 0))
        backward = [(target, source) for source, target in forward]
        low = lax.ppermute(
            lax.slice_in_dim(block, block.shape[dim] - width, None, axis=dim), axis, forward
        )
        high = lax.ppermute(lax.slice_in_dim(block, 0, width, axis=dim), axis, backward)
        block = jnp.concatenate([low, block, high], axis=dim)
    return block


def lookup(material, eps_table, grading):
    values = jnp.zeros(material.shape, jnp.float32)
    for index in range(eps_table.shape[0]):
        values = jnp.where(material == index, eps_table[index], values)
    return values * grading.astype(jnp.float32)


def box_mean(padded):
    total = padded[:-2] + padded[1:-1] + padded[2:]
    total = total[:, :-2] + total[:, 1:-1] + total[:, 2:]
    total = total[:, :, :-2] + total[:, :, 1:-1] + total[:, :, 2:]
    return total / 27.0


def tensor(mean_ext, mean_inv):
    centre = mean_ext[1:-1, 1:-1, 1:-1]
    grad_x = (mean_ext[2:, 1:-1, 1:-1] - mean_ext[:-2, 1:-1, 1:-1]) * 0.5
    grad_y = (mean_ext[1:-1, 2:, 1:-1] - mean_ext[1:-1, :-2, 1:-1]) * 0.5
    grad_z = (mean_ext[1:-1, 1:-1, 2:] - mean_ext[1:-1, 1:-1, :-2]) * 0.5
    scale = 1.0 / (grad_x * grad_x + grad_y * grad_y + grad_z * grad_z + 0.1)
    recip = 1.0 / centre
    grads = (grad_x, grad_y, grad_z)
    pairs = ((0, 0), (1, 1), (2, 2), (0, 1), (0, 2), (1, 2))
    result = []
    for first, second in pairs:
        weight = grads[first] * grads[second] * scale
        delta = 1.0 if first == second else 0.0
        result.append(mean_inv * weight + (delta - weight) * recip)
    return jnp.stack(result, 0).astype(jnp.bfloat16)


def local(material, eps_table, grading):
    eps = lookup(material, eps_table, grading)
    padded = padded_2(eps, (("gx", 0), ("gy", 1), ("gz", 2)), 2)
    mean_ext = box_mean(padded)
    mean_inv = box_mean(1.0 / padded[1:-1, 1:-1, 1:-1])
    return tensor(mean_ext, mean_inv)


def solution(mesh):
    return jax.shard_map(
        local,
        mesh=mesh,
        in_specs=(P("gx", "gy", "gz"), P(), P("gx", "gy", "gz")),
        out_specs=P(None, "gx", "gy", "gz"),
        check_vma=False,
    )
```

profile of v0, /device:TPU:0, one launch (start us, length us, event | category | flops | bytes accessed | tf_op | source)
XLA Modules:
  0.0 49.8 jit_solution(4201800438250576838)
XLA Ops:
  0.0 1.6 %fusion.23 = (f32[1]{0:T(128)}, f32[1]{0:T(128)}, f32[1]{0:T(128)}, f32[1]{0:T(128)}, f32[1]{0:T(128)}, /*index=5*/f32[1]{0:T(128)}, f32[1]{0:T(128)}, f32[1]{0:T(128)}) fusion(f32[8]{0:T(128)} %param.4), kind=kLoop, calls=%fused_computation.49 | loop fusion | bytes 64 | tf_op jit(solution)/shard_map/slice | solution.py:24
  1.6 7.0 %convert_multiply_fusion = f32[32,64,128]{2,1,0:T(8,128)S(1)} fusion(bf16[32,64,128]{2,1,0:T(8,128)(2,1)} %param.5, s32[32,64,128]{2,1,0:T(8,128)} %param.3, f32[]{:T(128)} %bitcast.7, f32[]{:T(128)} %bitcast.6, f32[]{:T(128)} %bitcast.5, f32[]{:T(128)} %bitcast.4, f32[]{:T(128)} %bitcast.3, f32[]{:T(128)} %bitcast.2, f32[]{:T(128)} %bitcast.1, f32[]{:T(128)} %bitcast), kind=kLoop, calls=%fused_computation.31 | loop fusion | flops 4718592 | bytes 2621472 | tf_op jit(solution)/shard_map/mul | solution.py:25
  8.6 3.0 %collective-permute-start = (f32[2,64,128]{2,1,0:T(8,128)S(1)}, f32[2,64,128]{2,1,0:T(8,128)S(1)}, u32[]{:S(2)}, u32[]{:S(2)}) collective-permute-start(f32[2,64,128]{2,1,0:T(8,128)S(1)} %get-tuple-element.14), channel_id=1, source_target_pairs={{0,8},{8,16},{16,24},{24,0},{1,9},{9,17},{17,25},{25,1},{2,10},{10... | collective-permute-start | bytes 196616 | tf_op jit(solution)/shard_map/ppermute | solution.py:13
  11.6 1.0 %collective-permute-start.1 = (f32[2,64,128]{2,1,0:T(8,128)S(1)}, f32[2,64,128]{2,1,0:T(8,128)S(1)}, u32[]{:S(2)}, u32[]{:S(2)}) collective-permute-start(f32[2,64,128]{2,1,0:T(8,128)S(1)} %get-tuple-element.15), channel_id=1, source_target_pairs={{8,0},{16,8},{24,16},{0,24},{9,1},{17,9},{25,17},{1,25},{10,2},{18... | collective-permute-start | bytes 196616 | tf_op jit(solution)/shard_map/ppermute | solution.py:16
  12.7 2.3 %collective-permute-done = f32[2,64,128]{2,1,0:T(8,128)S(1)} collective-permute-done((f32[2,64,128]{2,1,0:T(8,128)S(1)}, f32[2,64,128]{2,1,0:T(8,128)S(1)}, u32[]{:S(2)}, u32[]{:S(2)}) %collective-permute-start) | collective-permute-done | bytes 65568 | tf_op jit(solution)/shard_map/ppermute | solution.py:13
  14.9 1.4 %collective-permute-done.1 = f32[2,64,128]{2,1,0:T(8,128)S(1)} collective-permute-done((f32[2,64,128]{2,1,0:T(8,128)S(1)}, f32[2,64,128]{2,1,0:T(8,128)S(1)}, u32[]{:S(2)}, u32[]{:S(2)}) %collective-permute-start.1) | collective-permute-done | bytes 65568 | tf_op jit(solution)/shard_map/ppermute | solution.py:16
  16.4 1.6 %collective-permute-start.2 = (f32[36,2,128]{2,1,0:T(2,128)S(1)}, f32[36,2,128]{2,1,0:T(2,128)S(1)}, u32[]{:S(2)}, u32[]{:S(2)}) collective-permute-start(f32[36,2,128]{2,1,0:T(2,128)S(1)} %get-tuple-element.12), channel_id=1, source_target_pairs={{0,2},{2,4},{4,6},{6,0},{1,3},{3,5},{5,7},{7,1},{8,10},{10,12},{12... | collective-permute-start | bytes 110600 | tf_op jit(solution)/shard_map/ppermute | solution.py:13
  18.0 2.2 %collective-permute-start.3 = (f32[36,2,128]{2,1,0:T(2,128)S(1)}, f32[36,2,128]{2,1,0:T(2,128)S(1)}, u32[]{:S(2)}, u32[]{:S(2)}) collective-permute-start(f32[36,2,128]{2,1,0:T(2,128)S(1)} %get-tuple-element.13), channel_id=1, source_target_pairs={{2,0},{4,2},{6,4},{0,6},{3,1},{5,3},{7,5},{1,7},{10,8},{12,10},{14... | collective-permute-start | bytes 110600 | tf_op jit(solution)/shard_map/ppermute | solution.py:16
  20.2 2.0 %collective-permute-done.2 = f32[36,2,128]{2,1,0:T(2,128)S(1)} collective-permute-done((f32[36,2,128]{2,1,0:T(2,128)S(1)}, f32[36,2,128]{2,1,0:T(2,128)S(1)}, u32[]{:S(2)}, u32[]{:S(2)}) %collective-permute-start.2) | collective-permute-done | bytes 36896 | tf_op jit(solution)/shard_map/ppermute | solution.py:13
  22.5 1.5 %fusion.21 = (f32[36,68,2]{2,1,0:T(8,128)}, f32[36,68,2]{2,1,0:T(8,128)S(1)}) fusion(f32[36,68,128]{2,1,0:T(8,128)S(1)} %pad_maximum_fusion.1), kind=kLoop, calls=%fused_computation.47 | loop fusion | bytes 78336 | tf_op jit(solution)/shard_map/slice | solution.py:14
  24.0 1.8 %copy.14 = f32[36,68,2]{1,2,0:T(2,128)S(1)} copy(f32[36,68,2]{2,1,0:T(8,128)} %get-tuple-element.10) | data formatting | bytes 39168 | tf_op jit(solution)/shard_map/slice | solution.py:14
  26.3 0.5 %collective-permute-start.5 = (f32[36,68,2]{1,2,0:T(2,128)S(1)}, f32[36,68,2]{1,2,0:T(2,128)S(1)}, u32[]{:S(2)}, u32[]{:S(2)}) collective-permute-start(f32[36,68,2]{1,2,0:T(2,128)S(1)} %copy.15), channel_id=1, source_target_pairs={{1,0},{0,1},{3,2},{2,3},{5,4},{4,5},{7,6},{6,7},{9,8},{8,9},{11,10... | collective-permute-start | bytes 58760 | tf_op jit(solution)/shard_map/ppermute | solution.py:16
  27.0 0.6 %copy.16 = f32[36,68,2]{2,1,0:T(8,128)S(1)} copy(f32[36,68,2]{1,2,0:T(2,128)S(1)} %collective-permute-done.4) | data formatting | bytes 39168 | tf_op jit(solution)/shard_map/ppermute | solution.py:13
  27.8 1.6 %copy.17 = f32[36,68,2]{2,1,0:T(8,128)} copy(f32[36,68,2]{1,2,0:T(2,128)S(1)} %collective-permute-done.5) | data formatting | bytes 39168 | tf_op jit(solution)/shard_map/ppermute | solution.py:16
  29.3 2.6 %pad_maximum_fusion = f32[36,68,132]{2,1,0:T(8,128)S(1)} fusion(f32[36,68,2]{2,1,0:T(8,128)} %copy.17, f32[36,2,128]{2,1,0:T(2,128)S(1)} %collective-permute-done.3, f32[2,64,128]{2,1,0:T(8,128)S(1)} %collective-permute-done.1, f32[32,64,128]{2,1,0:T(8,128)S(1)} %convert_multiply_fusion, f32[2,64,128]{2,1,0:T(8,128)S(1)} %collective-permute-done, ...), kind=kLoop, calls=%fused_computation | loop fusion | flops 1938816 | bytes 2585088 | tf_op jit(solution)/shard_map/concatenate | solution.py:17
  32.1 0.8 %slice_divide_fusion = f32[34,66,130]{2,1,0:T(8,128)S(1)} fusion(f32[36,68,132]{2,1,0:T(8,128)S(1)} %pad_maximum_fusion), kind=kLoop, calls=%fused_computation.8 | loop fusion | flops 291720 | bytes 2333760 | tf_op jit(solution)/shard_map/div | solution.py:56
  33.1 1.7 %slice_add_fusion.8 = f32[32,64,130]{2,1,0:T(8,128)} fusion(f32[32,66,130]{2,1,0:T(8,128)S(1)} %slice_add_fusion.6), kind=kLoop, calls=%fused_computation.11 | loop fusion | flops 532480 | bytes 4259840 | tf_op jit(solution)/shard_map/add | solution.py:30
  35.4 1.4 %fusion = f32[34,66,130]{2,1,0:T(8,128)S(1)} fusion(f32[34,66,132]{2,1,0:T(8,128)S(1)} %slice_add_fusion.2), kind=kLoop, calls=%fused_computation.2 | loop fusion | flops 875160 | bytes 4667520 | tf_op jit(solution)/shard_map/div | solution.py:32
  36.7 5.6 %fusion.6 = (bf16[6,32,64,128]{3,2,1,0:T(8,128)(2,1)}, f32[32,64,128]{2,1,0:T(8,128)S(1)}, f32[32,64,128]{2,1,0:T(8,128)S(1)}, f32[32,64,128]{2,1,0:T(8,128)S(1)}, f32[32,64,128]{2,1,0:T(8,128)S(1)}) fusion(f32[34,66,130]{2,1,0:T(8,128)S(1)} %fusion, f32[32,64,130]{2,1,0:T(8,128)} %slice_add_fusion.8), kind=kLoop, calls=%fused_computation.33 | loop fusion | flops 6029311 | bytes 15204352
  42.4 1.5 %fusion.8 = bf16[6,32,64,128]{3,2,1,0:T(8,128)(2,1)} fusion(bf16[6,32,64,128]{3,2,1,0:T(8,128)(2,1)} %get-tuple-element.5, f32[32,64,128]{2,1,0:T(8,128)S(1)} %get-tuple-element.9, f32[32,64,128]{2,1,0:T(8,128)S(1)} %get-tuple-element.6, f32[34,66,130]{2,1,0:T(8,128)S(1)} %fusion, f32[32,64,128]{2,1,0:T(8,128)S(1)} %get-tuple-element.7, ...), kind=kLoop, calls=%fused_computation.35 | loop fusion | flops 3670016 | bytes 5767168
  43.8 1.5 %fusion.10 = bf16[6,32,64,128]{3,2,1,0:T(8,128)(2,1)} fusion(bf16[6,32,64,128]{3,2,1,0:T(8,128)(2,1)} %fusion.8, f32[32,64,128]{2,1,0:T(8,128)S(1)} %get-tuple-element.9, f32[32,64,128]{2,1,0:T(8,128)S(1)} %get-tuple-element.7, f32[34,66,130]{2,1,0:T(8,128)S(1)} %fusion, f32[32,64,128]{2,1,0:T(8,128)S(1)} %get-tuple-element.6, ...), kind=kLoop, calls=%fused_computation.37 | loop fusion | flops 3670016 | bytes 5767168
  45.3 1.5 %fusion.12 = bf16[6,32,64,128]{3,2,1,0:T(8,128)(2,1)} fusion(bf16[6,32,64,128]{3,2,1,0:T(8,128)(2,1)} %fusion.10, f32[32,64,128]{2,1,0:T(8,128)S(1)} %get-tuple-element.9, f32[32,64,128]{2,1,0:T(8,128)S(1)} %get-tuple-element.8, f32[32,64,128]{2,1,0:T(8,128)S(1)} %get-tuple-element.6, f32[34,66,130]{2,1,0:T(8,128)S(1)} %fusion, ...), kind=kLoop, calls=%fused_computation.39 | loop fusion | flops 3932160 | bytes 5767168
  46.8 1.5 %fusion.14 = bf16[6,32,64,128]{3,2,1,0:T(8,128)(2,1)} fusion(bf16[6,32,64,128]{3,2,1,0:T(8,128)(2,1)} %fusion.12, f32[32,64,128]{2,1,0:T(8,128)S(1)} %get-tuple-element.9, f32[32,64,128]{2,1,0:T(8,128)S(1)} %get-tuple-element.8, f32[32,64,128]{2,1,0:T(8,128)S(1)} %get-tuple-element.7, f32[34,66,130]{2,1,0:T(8,128)S(1)} %fusion, ...), kind=kLoop, calls=%fused_computation.41 | loop fusion | flops 3932160 | bytes 5767168
  48.3 1.5 %fusion.16 = bf16[6,32,64,128]{3,2,1,0:T(8,128)(2,1)} fusion(bf16[6,32,64,128]{3,2,1,0:T(8,128)(2,1)} %fusion.14, f32[32,64,128]{2,1,0:T(8,128)S(1)} %get-tuple-element.9, f32[32,64,128]{2,1,0:T(8,128)S(1)} %get-tuple-element.6, f32[32,64,128]{2,1,0:T(8,128)S(1)} %get-tuple-element.7, f32[34,66,130]{2,1,0:T(8,128)S(1)} %fusion, ...), kind=kLoop, calls=%fused_computation.43 | loop fusion | flops 3932160 | bytes 5767168 | tf_op jit(solution)/shard_map/stack | solution.py:49
  (11 shorter events, 2.0 us)
Async XLA Ops:
  8.6 6.3 %collective-permute-start = (f32[2,64,128]{2,1,0:T(8,128)S(1)}, f32[2,64,128]{2,1,0:T(8,128)S(1)}, u32[]{:S(2)}, u32[]{:S(2)}) collective-permute-start(f32[2,64,128]{2,1,0:T(8,128)S(1)} %get-tuple-element.14), channel_id=1, source_target_pairs={{0,8},{8,16},{16,24},{24,0},{1,9},{9,17},{17,25},{25,1},{2,10},{10... | collective-permute-start | bytes 196616 | tf_op jit(solution)/shard_map/ppermute | solution.py:13
  11.6 4.7 %collective-permute-start.1 = (f32[2,64,128]{2,1,0:T(8,128)S(1)}, f32[2,64,128]{2,1,0:T(8,128)S(1)}, u32[]{:S(2)}, u32[]{:S(2)}) collective-permute-start(f32[2,64,128]{2,1,0:T(8,128)S(1)} %get-tuple-element.15), channel_id=1, source_target_pairs={{8,0},{16,8},{24,16},{0,24},{9,1},{17,9},{25,17},{1,25},{10,2},{18... | collective-permute-start | bytes 196616 | tf_op jit(solution)/shard_map/ppermute | solution.py:16
  16.4 5.9 %collective-permute-start.2 = (f32[36,2,128]{2,1,0:T(2,128)S(1)}, f32[36,2,128]{2,1,0:T(2,128)S(1)}, u32[]{:S(2)}, u32[]{:S(2)}) collective-permute-start(f32[36,2,128]{2,1,0:T(2,128)S(1)} %get-tuple-element.12), channel_id=1, source_target_pairs={{0,2},{2,4},{4,6},{6,0},{1,3},{3,5},{5,7},{7,1},{8,10},{10,12},{12... | collective-permute-start | bytes 110600 | tf_op jit(solution)/shard_map/ppermute | solution.py:13
  18.0 4.4 %collective-permute-start.3 = (f32[36,2,128]{2,1,0:T(2,128)S(1)}, f32[36,2,128]{2,1,0:T(2,128)S(1)}, u32[]{:S(2)}, u32[]{:S(2)}) collective-permute-start(f32[36,2,128]{2,1,0:T(2,128)S(1)} %get-tuple-element.13), channel_id=1, source_target_pairs={{2,0},{4,2},{6,4},{0,6},{3,1},{5,3},{7,5},{1,7},{10,8},{12,10},{14... | collective-permute-start | bytes 110600 | tf_op jit(solution)/shard_map/ppermute | solution.py:16
  25.8 1.3 %collective-permute-start.4 = (f32[36,68,2]{1,2,0:T(2,128)S(1)}, f32[36,68,2]{1,2,0:T(2,128)S(1)}, u32[]{:S(2)}, u32[]{:S(2)}) collective-permute-start(f32[36,68,2]{1,2,0:T(2,128)S(1)} %copy.14), channel_id=1, source_target_pairs={{0,1},{1,0},{2,3},{3,2},{4,5},{5,4},{6,7},{7,6},{8,9},{9,8},{10,11... | collective-permute-start | bytes 58760 | tf_op jit(solution)/shard_map/ppermute | solution.py:13
  26.3 1.4 %collective-permute-start.5 = (f32[36,68,2]{1,2,0:T(2,128)S(1)}, f32[36,68,2]{1,2,0:T(2,128)S(1)}, u32[]{:S(2)}, u32[]{:S(2)}) collective-permute-start(f32[36,68,2]{1,2,0:T(2,128)S(1)} %copy.15), channel_id=1, source_target_pairs={{1,0},{0,1},{3,2},{2,3},{5,4},{4,5},{7,6},{6,7},{9,8},{8,9},{11,10... | collective-permute-start | bytes 58760 | tf_op jit(solution)/shard_map/ppermute | solution.py:16
where the time goes:
time: 50.1 us; the launch traced here: 49.8 us
  other arithmetic  27.6 us (55%)
  starting transfers between devices  8.54 us (17%)
  local copies, waits for them, and re-layouts  7.55 us (15%)
  waiting for transfers between devices  6.07 us (12%)
    unnamed x5, other arithmetic  11.6 us
    mul x1, other arithmetic, lookup(): return values * grading.astype(jnp.float32)  6.98 us
    ppermute x3, starting transfers between devices, padded_2(): lax.ppermute(lax.slice_in_dim(block, block.shape[dim] - width, None, axis...  4.72 us
    ppermute x3, waiting for transfers between devices, padded_2(): lax.ppermute(lax.slice_in_dim(block, block.shape[dim] - width, None, axis...  4.47 us
    ppermute x3, starting transfers between devices, padded_2(): lax.ppermute(lax.slice_in_dim(block, 0, width, axis=dim), axis, backward)  3.82 us
    slice x3, local copies, waits for them, and re-layouts, padded_2(): lax.slice_in_dim(block, block.shape[dim] - width, None, axis=dim)  3.28 us
    concatenate x2, other arithmetic, padded_2(): block = jnp.concatenate([low, block, high], axis=dim)  2.73 us
    add x2, other arithmetic, box_mean(): total = total[:, :-2] + total[:, 1:-1] + total[:, 2:]  2.23 us
  transfers between devices with their start and end apart: 6, of which 6 were waited for; matrix products, arithmetic and copies ran while one was open for 2% of the time, Pallas kernels for 0%

commit v1 on v0

v1 whole, which is shorter than its diff:
```python
import functools

import jax
import jax.numpy as jnp
from jax import lax
from jax.experimental import pallas as pl
from jax.experimental.pallas import tpu as pltpu
from jax.sharding import PartitionSpec as P

MESH = pl.DeviceIdType.MESH
CHUNKS = 4
PAD = 8


def inverse(x):
    guess = pl.reciprocal(x, approx=True)
    return guess * (2.0 - x * guess)


def kernel(nx, ny, nz, X, Y, mat_hbm, table, grad_hbm, out, mat, grad, eps, peer, halo, halo_peer, faces,
           zs, zd, zi, in_sem, main_send, main_recv, face_send, face_recv, fwd_send, fwd_recv):
    Z = mat.shape[-1]
    zpeers = 1 if nz == 2 else 2
    xs, ys = 2 * Y, 2 * X
    pieces = ((0, xs), (xs, xs), (2 * xs, ys), (2 * xs + ys, ys)) + tuple(
        (2 * xs + 2 * ys + 8 * c, 8) for c in range(4)
    )
    rows = X * Y // CHUNKS

    def load(c):
        part = pl.ds(c * rows, rows)
        return (
            pltpu.make_async_copy(mat_hbm.at[part], mat.at[part], in_sem.at[0, c]),
            pltpu.make_async_copy(grad_hbm.at[part], grad.at[part], in_sem.at[1, c]),
        )

    order = (0, CHUNKS - 1) + tuple(range(1, CHUNKS - 1))
    for c in order:
        for copy in load(c):
            copy.start()

    me = (lax.axis_index("gx"), lax.axis_index("gy"), lax.axis_index("gz"))
    sizes = (nx, ny, nz)

    def near(*steps):
        return tuple(
            me[k] if d == 0 else lax.rem(me[k] + (d + sizes[k]), sizes[k]) for k, d in enumerate(steps)
        )

    zdevs = [near(0, 0, 1), near(0, 0, -1)][:zpeers]
    around = [near(i, j, 0) for i in (-1, 0, 1) for j in (-1, 0, 1) if (i, j) != (0, 0)]
    barrier = pltpu.get_barrier_semaphore()
    for dev in around + zdevs:
        pl.semaphore_signal(barrier, inc=1, device_id=dev, device_id_type=MESH)

    values = [table[k] for k in range(table.shape[0])]

    def look(c):
        for copy in load(c):
            copy.wait()

        def plane(i, carry):
            part = pl.ds(pl.multiple_of(c * rows + i * Y, Y), Y)
            m = mat[part]
            v = jnp.full(m.shape, values[0], jnp.float32)
            for k in range(1, len(values)):
                v = jnp.where(m == k, values[k], v)
            eps[part] = v * grad[part].astype(jnp.float32)
            return carry

        lax.fori_loop(0, rows // Y, plane, 0)

    def main_copy(c, side):
        part = pl.ds(c * rows, rows)
        return pltpu.make_async_remote_copy(
            eps.at[part], peer.at[side, part], main_send.at[side, c], main_recv.at[side, c],
            device_id=zdevs[side], device_id_type=MESH,
        )

    def piece(ref, k):
        return ref.at[pl.ds(pieces[k][0], pieces[k][1])]

    def face_copy(k, src, dev):
        return pltpu.make_async_remote_copy(
            src, piece(halo, k), face_send.at[k], face_recv.at[k], device_id=dev, device_id_type=MESH
        )

    def forward(k, side):
        start, count = pieces[k]
        return pltpu.make_async_remote_copy(
            piece(halo, k), halo_peer.at[side, pl.ds(start, count)], fwd_send.at[side, k],
            fwd_recv.at[side, k], device_id=zdevs[side], device_id_type=MESH,
        )

    edges = 2 * ys
    copies = {
        1: face_copy(1, eps.at[pl.ds(0, xs)], near(-1, 0, 0)),
        0: face_copy(0, eps.at[pl.ds(X * Y - xs, xs)], near(1, 0, 0)),
        3: face_copy(3, faces.at[pl.ds(0, ys)], near(0, -1, 0)),
        2: face_copy(2, faces.at[pl.ds(ys, ys)], near(0, 1, 0)),
    }
    for sx in range(2):
        for sy in range(2):
            mine, theirs = 2 * sx + sy, 2 * (1 - sx) + (1 - sy)
            copies[4 + theirs] = face_copy(
                4 + theirs, faces.at[pl.ds(edges + 8 * mine, 8)], near(2 * sx - 1, 2 * sy - 1, 0)
            )
    mains = {(c, s): main_copy(c, s) for c in order for s in range(zpeers)}
    forwards = {(k, s): forward(k, s) for k in range(8) for s in range(zpeers)}

    for c in order[:2]:
        look(c)
    pl.semaphore_wait(barrier, len(around) + len(zdevs))
    copies[0].start()
    copies[1].start()
    for c in order[2:]:
        look(c)
    for l in range(2):
        for side in range(2):
            y = l if side == 0 else Y - 2 + l
            faces[pl.ds(side * ys + l * X, X)] = eps[pl.ds(y, X, stride=Y)]
    faces[pl.ds(edges, 32)] = jnp.ones((32, Z), jnp.float32)
    for sx in range(2):
        for sy in range(2):
            for a in range(2):
                x, y = (X - 2) * sx + a, (Y - 2) * sy
                faces[pl.ds(edges + 8 * (2 * sx + sy) + 2 * a, 2)] = eps[pl.ds(x * Y + y, 2)]
    for c in order:
        for s in range(zpeers):
            mains[c, s].start()
    for k in range(4, 8):
        copies[k].start()
    for k in (2, 3):
        copies[k].start()

    def zfilter(e, low, high):
        lane = lax.broadcasted_iota(jnp.int32, e.shape, 1)
        m1 = pltpu.roll(jnp.where(lane == Z - 1, low, e), 1, 1)
        m2 = pltpu.roll(jnp.where(lane >= Z - 2, low, e), 2, 1)
        p1 = pltpu.roll(jnp.where(lane == 0, high, e), Z - 1, 1)
        p2 = pltpu.roll(jnp.where(lane < 2, high, e), Z - 2, 1)
        both, prod = m1 + p1, m1 * p1
        return e + both, (p1 - m1) + (p2 - m2), (prod + e * both) * inverse(e * prod)

    def sides(ref, part):
        low = ref[0, part]
        return low, (low if zpeers == 1 else ref[1, part])

    for c in order:
        for s in range(zpeers):
            mains[c, s].wait_recv()

        def plane(i, carry):
            x = c * (rows // Y) + i
            part = pl.ds(pl.multiple_of(x * Y, Y), Y)
            for ref, value in zip((zs, zd, zi), zfilter(eps[part], *sides(peer, part))):
                ref[x + 2, PAD:PAD + Y] = value
            return carry

        lax.fori_loop(0, rows // Y, plane, 0)

    def yrows(ref, p, j, shift):
        return ref[p, PAD + 16 * j + shift:PAD + 16 * j + shift + 16]

    def lead(p, j):
        a, b = yrows(zs, p, j, -1), yrows(zs, p, j, 1)
        return yrows(zs, p, j, 0) + (a + b)

    def rest(p, j):
        b = (yrows(zs, p, j, 1) - yrows(zs, p, j, -1)) + (yrows(zs, p, j, 2) - yrows(zs, p, j, -2))
        return b, sum(yrows(zd, p, j, k) for k in (-1, 0, 1)), sum(yrows(zi, p, j, k) for k in (-1, 0, 1))

    def outputs(j, start, count, unroll):
        def step(x, carry):
            (a0, a1, a2, a3), r0, r1 = carry
            a4 = lead(x + 4, j)
            r2 = rest(x + 3, j)
            total = a2 + (a1 + a3)
            gx = (a3 - a1) + (a4 - a0)
            gy, gz, inv = (u + v + w for u, v, w in zip(r0, r1, r2))
            den = gx * gx + gy * gy + gz * gz + 291.6
            q = inverse(total * den)
            recip = (den * q) * 27.0
            k = (inv * (1.0 / 27.0) - recip) * (total * q)
            kx, ky, kz = gx * k, gy * k, gz * k
            result = (gx * kx + recip, gy * ky + recip, gz * kz + recip, gx * ky, gx * kz, gy * kz)
            for n, value in enumerate(result):
                out[n, x, 16 * j:16 * j + 16] = value.astype(out.dtype)
            return (a1, a2, a3, a4), r1, r2

        carry = (tuple(lead(start + k, j) for k in range(4)), rest(start + 1, j), rest(start + 2, j))
        if count == unroll:
            for k in range(count):
                carry = step(start + k, carry)
        else:
            def block(i, carry):
                for k in range(unroll):
                    carry = step(start + i * unroll + k, carry)
                return carry

            lax.fori_loop(0, count // unroll, block, carry)

    def arrive(ks):
        for k in ks:
            copies[k].wait_recv()
            for s in range(zpeers):
                forwards[k, s].start()

    def halo_filter(k):
        for s in range(zpeers):
            forwards[k, s].wait_recv()
        part = pl.ds(*pieces[k])
        fields = zfilter(halo[part], *sides(halo_peer, part))
        for ref, value in zip((zs, zd, zi), fields):
            if k < 2:
                p = k * (X + 2)
                ref[p, PAD:PAD + Y] = value[:Y]
                ref[p + 1, PAD:PAD + Y] = value[Y:]
            elif k < 4:
                flat = ref.reshape((X + 4) * (Y + 2 * PAD), Z)
                y = PAD - 2 if k == 2 else PAD + Y
                for l in range(2):
                    flat[pl.ds(2 * (Y + 2 * PAD) + y + l, X, stride=Y + 2 * PAD)] = value[l * X:(l + 1) * X]
            else:
                sx, sy = divmod(k - 4, 2)
                y = PAD - 2 if sy == 0 else PAD + Y
                for a in range(2):
                    ref[sx * (X + 2) + a, y:y + 2] = value[2 * a:2 * a + 2]

    pairs = Y // 16
    unroll = 4
    inside = range(1, pairs - 1)
    for n, j in enumerate(inside):
        outputs(j, 2, X - 4, unroll)
        if n == 0:
            arrive((2, 3))
    arrive((0, 1, 4, 5, 6, 7))
    halo_filter(2)
    halo_filter(3)
    outputs(0, 2, X - 4, unroll)
    outputs(pairs - 1, 2, X - 4, unroll)
    for k in (0, 1, 4, 5, 6, 7):
        halo_filter(k)
    for j in range(pairs):
        outputs(j, 0, 2, 2)
        outputs(j, X - 2, 2, 2)
    for copy in list(copies.values()) + list(mains.values()) + list(forwards.values()):
        copy.wait_send()


def solution(mesh):
    nx, ny, nz = mesh.shape["gx"], mesh.shape["gy"], mesh.shape["gz"]

    def local(material, eps_table, grading):
        X, Y, Z = material.shape
        zpeers = 1 if nz == 2 else 2
        halo_rows = 4 * Y + 4 * X + 32
        any_space = pl.BlockSpec(memory_space=pl.ANY)
        dma = pltpu.SemaphoreType.DMA
        field = pltpu.VMEM((X + 4, Y + 2 * PAD, Z), jnp.float32)
        return pl.pallas_call(
            functools.partial(kernel, nx, ny, nz, X, Y),
            out_shape=jax.ShapeDtypeStruct((6, X, Y, Z), jnp.bfloat16),
            in_specs=[any_space, pl.BlockSpec(memory_space=pltpu.SMEM), any_space],
            out_specs=pl.BlockSpec(memory_space=pltpu.VMEM),
            scratch_shapes=[
                pltpu.VMEM((X * Y, Z), jnp.int32),
                pltpu.VMEM((X * Y, Z), jnp.bfloat16),
                pltpu.VMEM((X * Y, Z), jnp.float32),
                pltpu.VMEM((zpeers, X * Y, Z), jnp.float32),
                pltpu.VMEM((halo_rows, Z), jnp.float32),
                pltpu.VMEM((zpeers, halo_rows, Z), jnp.float32),
                pltpu.VMEM((4 * X + 32, Z), jnp.float32),
                field, field, field,
                dma((2, CHUNKS)),
                dma((zpeers, CHUNKS)), dma((zpeers, CHUNKS)),
                dma((8,)), dma((8,)),
                dma((zpeers, 8)), dma((zpeers, 8)),
            ],
            compiler_params=pltpu.CompilerParams(collective_id=0, has_side_effects=True),
        )(material.reshape(X * Y, Z), eps_table, grading.reshape(X * Y, Z))

    return jax.shard_map(
        local,
        mesh=mesh,
        in_specs=(P("gx", "gy", "gz"), P(), P("gx", "gy", "gz")),
        out_specs=P(None, "gx", "gy", "gz"),
        check_vma=False,
    )
```

time: 50.1 us -> 23.3 us (0.47)
  other arithmetic: 27.6 us -> 0 us
  Pallas kernels: 0 us -> 18.4 us
  starting transfers between devices: 8.54 us -> 0 us
  waiting for transfers between devices: 6.07 us -> 0 us
  local copies, waits for them, and re-layouts: 7.55 us -> 4.7 us
    pallas_call x0 -> x1, Pallas kernels: none -> 18.4 us  [local(): pl.pallas_call(functools.partial(kernel, nx, ny, nz, X, Y), out_shape=jax...]
    unnamed x5 -> x0, other arithmetic: 11.6 us -> none
    ppermute x6 -> x0, starting transfers between devices: 8.54 us -> none  [the longest x3 4.72 us: padded_2(): lax.ppermute(lax.slice_in_dim(block, block.shape[dim] - width, None, axis...]
    mul x1 -> x0, other arithmetic: 6.98 us -> none  [lookup(): return values * grading.astype(jnp.float32)]
    ppermute x6 -> x0, waiting for transfers between devices: 6.07 us -> none  [the longest x3 4.47 us: padded_2(): lax.ppermute(lax.slice_in_dim(block, block.shape[dim] - width, None, axis...]
    slice x5 -> x0, local copies, waits for them, and re-layouts: 5.38 us -> none  [the longest x3 3.28 us: padded_2(): lax.slice_in_dim(block, block.shape[dim] - width, None, axis=dim)]
    unnamed x0 -> x1, local copies, waits for them, and re-layouts: none -> 4.7 us
    concatenate x2 -> x0, other arithmetic: 2.73 us -> none  [padded_2(): block = jnp.concatenate([low, block, high], axis=dim)]
  transfers between devices with their start and end apart: 6 -> 0, of which waited for: 6 -> 0; matrix products, arithmetic and copies ran while one was open for 2% -> 0% of each run, Pallas kernels for 0% -> 0%
where the time goes in v1:
time: 23.3 us; the launch traced here: 23.1 us
  Pallas kernels  18.4 us (79%)
  local copies, waits for them, and re-layouts  4.7 us (20%)
    pallas_call x1, Pallas kernels, local(): pl.pallas_call(functools.partial(kernel, nx, ny, nz, X, Y), out_shape=jax...  18.4 us
    unnamed x1, local copies, waits for them, and re-layouts  4.7 us

profile of v1, /device:TPU:0, one launch (start us, length us, event | category | flops | bytes accessed | tf_op | source)
XLA Modules:
  0.0 23.1 jit_solution(7254214963717452677)
XLA Ops:
  0.0 18.4 %shard_map.37 = bf16[6,32,64,128]{3,2,1,0:T(8,128)(2,1)} custom-call(s32[2048,128]{1,0:T(8,128)} %bitcast.2, f32[8]{0:T(128)} %table.1, bf16[2048,128]{1,0:T(8,128)(2,1)} %bitcast.3), custom_call_target="tpu_custom_call" | custom-call | tf_op jit(solution)/shard_map/pallas_call | solution.py:261
  18.4 4.7 %copy.5 = bf16[6,32,64,128]{3,2,1,0:T(8,128)(2,1)} copy(bf16[6,32,64,128]{3,2,1,0:T(8,128)(2,1)} %shard_map.37) | data formatting | bytes 6291456

commit v2 on v1

--- a/solution.py
+++ b/solution.py
@@ -17,8 +17,8 @@
     return guess * (2.0 - x * guess)
 
 
-def kernel(nx, ny, nz, X, Y, mat_hbm, table, grad_hbm, out, mat, grad, eps, peer, halo, halo_peer, faces,
-           zs, zd, zi, in_sem, main_send, main_recv, face_send, face_recv, fwd_send, fwd_recv):
+def kernel(nx, ny, nz, X, Y, mat_hbm, table_hbm, grad_hbm, out, mat, table, grad, eps, peer, halo, halo_peer, faces,
+           zs, zd, zi, in_sem, table_sem, main_send, main_recv, face_send, face_recv, fwd_send, fwd_recv):
     Z = mat.shape[-1]
     zpeers = 1 if nz == 2 else 2
     xs, ys = 2 * Y, 2 * X
@@ -35,6 +35,8 @@
         )
 
     order = (0, CHUNKS - 1) + tuple(range(1, CHUNKS - 1))
+    table_copy = pltpu.make_async_copy(table_hbm, table, table_sem)
+    table_copy.start()
     for c in order:
         for copy in load(c):
             copy.start()
@@ -53,6 +55,7 @@
     for dev in around + zdevs:
         pl.semaphore_signal(barrier, inc=1, device_id=dev, device_id_type=MESH)
 
+    table_copy.wait()
     values = [table[k] for k in range(table.shape[0])]
 
     def look(c):
@@ -248,6 +251,14 @@
         copy.wait_send()
 
 
+def write_out(result, out, sem):
+    copies = [pltpu.make_async_copy(result.at[n], out.at[n], sem.at[n]) for n in range(out.shape[0])]
+    for copy in copies:
+        copy.start()
+    for copy in copies:
+        copy.wait()
+
+
 def solution(mesh):
     nx, ny, nz = mesh.shape["gx"], mesh.shape["gy"], mesh.shape["gz"]
 
@@ -258,13 +269,14 @@
         any_space = pl.BlockSpec(memory_space=pl.ANY)
         dma = pltpu.SemaphoreType.DMA
         field = pltpu.VMEM((X + 4, Y + 2 * PAD, Z), jnp.float32)
-        return pl.pallas_call(
+        result = pl.pallas_call(
             functools.partial(kernel, nx, ny, nz, X, Y),
-            out_shape=jax.ShapeDtypeStruct((6, X, Y, Z), jnp.bfloat16),
-            in_specs=[any_space, pl.BlockSpec(memory_space=pltpu.SMEM), any_space],
+            out_shape=pltpu.VMEM((6, X, Y, Z), jnp.bfloat16),
+            in_specs=[pl.BlockSpec(memory_space=pltpu.HBM)] * 3,
             out_specs=pl.BlockSpec(memory_space=pltpu.VMEM),
             scratch_shapes=[
                 pltpu.VMEM((X * Y, Z), jnp.int32),
+                pltpu.SMEM(eps_table.shape, jnp.float32),
                 pltpu.VMEM((X * Y, Z), jnp.bfloat16),
                 pltpu.VMEM((X * Y, Z), jnp.float32),
                 pltpu.VMEM((zpeers, X * Y, Z), jnp.float32),
@@ -272,13 +284,24 @@
                 pltpu.VMEM((zpeers, halo_rows, Z), jnp.float32),
                 pltpu.VMEM((4 * X + 32, Z), jnp.float32),
                 field, field, field,
-                dma((2, CHUNKS)),
+                dma((2, CHUNKS)), dma(()),
                 dma((zpeers, CHUNKS)), dma((zpeers, CHUNKS)),
                 dma((8,)), dma((8,)),
                 dma((zpeers, 8)), dma((zpeers, 8)),
             ],
-            compiler_params=pltpu.CompilerParams(collective_id=0, has_side_effects=True),
-        )(material.reshape(X * Y, Z), eps_table, grading.reshape(X * Y, Z))
+            compiler_params=pltpu.CompilerParams(
+                collective_id=0, has_side_effects=True, vmem_limit_bytes=24 * 2**20
+            ),
+        )(*(pltpu.with_memory_space_constraint(a, pltpu.HBM)
+            for a in (material.reshape(X * Y, Z), eps_table, grading.reshape(X * Y, Z))))
+        return pl.pallas_call(
+            write_out,
+            out_shape=jax.ShapeDtypeStruct((6, X, Y, Z), jnp.bfloat16),
+            in_specs=[pl.BlockSpec(memory_space=pltpu.VMEM)],
+            out_specs=any_space,
+            scratch_shapes=[dma((6,))],
+            compiler_params=pltpu.CompilerParams(vmem_limit_bytes=24 * 2**20),
+        )(result)
 
     return jax.shard_map(
         local,

time: 23.3 us -> 17.9 us (0.77)
  local copies, waits for them, and re-layouts: 4.7 us -> 0 us
  Pallas kernels: 18.4 us -> 17.7 us
    unnamed x1 -> x0, local copies, waits for them, and re-layouts: 4.7 us -> none
    pallas_call x1 -> x2, Pallas kernels: 18.4 us -> 17.7 us  [the longest x1 16 us: local(): pl.pallas_call(functools.partial(kernel, nx, ny, nz, X, Y), out_shape=plt...]
where the time goes in v2:
time: 17.9 us; the launch traced here: 17.7 us
  Pallas kernels  17.7 us (99%)
    pallas_call x1, Pallas kernels, local(): pl.pallas_call(functools.partial(kernel, nx, ny, nz, X, Y), out_shape=plt...  16 us
    pallas_call x1, Pallas kernels, local(): pl.pallas_call(write_out, out_shape=jax.ShapeDtypeStruct((6, X, Y, Z), jn...  1.71 us

profile of v2, /device:TPU:0, one launch (start us, length us, event | category | flops | bytes accessed | tf_op | source)
XLA Modules:
  0.0 17.7 jit_solution(18291958628781382039)
XLA Ops:
  0.0 16.0 %shard_map.37.result = bf16[6,32,64,128]{3,2,1,0:T(8,128)(2,1)S(1)} custom-call(s32[2048,128]{1,0:T(8,128)} %bitcast.2, f32[8]{0:T(128)} %table_hbm.1, bf16[2048,128]{1,0:T(8,128)(2,1)} %bitcast.3), custom_call_target="tpu_custom_call" | custom-call | tf_op jit(solution)/shard_map/pallas_call | solution.py:272
  16.0 1.7 %shard_map.38 = bf16[6,32,64,128]{3,2,1,0:T(8,128)(2,1)} custom-call(bf16[6,32,64,128]{3,2,1,0:T(8,128)(2,1)S(1)} %shard_map.37.result), custom_call_target="tpu_custom_call" | custom-call | tf_op jit(solution)/shard_map/pallas_call | solution.py:297

commit v3 on v2

--- a/solution.py
+++ b/solution.py
@@ -18,7 +18,7 @@
 
 
 def kernel(nx, ny, nz, X, Y, mat_hbm, table_hbm, grad_hbm, out, mat, table, grad, eps, peer, halo, halo_peer, faces,
-           zs, zd, zi, in_sem, table_sem, main_send, main_recv, face_send, face_recv, fwd_send, fwd_recv):
+           zs, zd, zi, in_sem, table_sem, main_send, main_recv, face_send, face_recv, fwd_send, fwd_recv, entered):
     Z = mat.shape[-1]
     zpeers = 1 if nz == 2 else 2
     xs, ys = 2 * Y, 2 * X
@@ -35,25 +35,26 @@
         )
 
     order = (0, CHUNKS - 1) + tuple(range(1, CHUNKS - 1))
+    me = (lax.axis_index("gx"), lax.axis_index("gy"), lax.axis_index("gz"))
+    sizes = (nx, ny, nz)
+
+    def near(*steps):
+        return tuple(
+            me[k] if d == 0 else lax.rem(me[k] + (d + sizes[k]), sizes[k]) for k, d in enumerate(steps)
+        )
+
+    zdevs = [near(0, 0, 1), near(0, 0, -1)][:zpeers]
+    xdevs = [near(-1, 0, 0), near(1, 0, 0)]
+    around = [near(0, -1, 0), near(0, 1, 0)] + xdevs
+    barrier = pltpu.get_barrier_semaphore()
+    for dev in around + zdevs:
+        pl.semaphore_signal(barrier, inc=1, device_id=dev, device_id_type=MESH)
+
     table_copy = pltpu.make_async_copy(table_hbm, table, table_sem)
     table_copy.start()
     for c in order:
         for copy in load(c):
             copy.start()
-
-    me = (lax.axis_index("gx"), lax.axis_index("gy"), lax.axis_index("gz"))
-    sizes = (nx, ny, nz)
-
-    def near(*steps):
-        return tuple(
-            me[k] if d == 0 else lax.rem(me[k] + (d + sizes[k]), sizes[k]) for k, d in enumerate(steps)
-        )
-
-    zdevs = [near(0, 0, 1), near(0, 0, -1)][:zpeers]
-    around = [near(i, j, 0) for i in (-1, 0, 1) for j in (-1, 0, 1) if (i, j) != (0, 0)]
-    barrier = pltpu.get_barrier_semaphore()
-    for dev in around + zdevs:
-        pl.semaphore_signal(barrier, inc=1, device_id=dev, device_id_type=MESH)
 
     table_copy.wait()
     values = [table[k] for k in range(table.shape[0])]
@@ -111,12 +112,7 @@
     mains = {(c, s): main_copy(c, s) for c in order for s in range(zpeers)}
     forwards = {(k, s): forward(k, s) for k in range(8) for s in range(zpeers)}
 
-    for c in order[:2]:
-        look(c)
-    pl.semaphore_wait(barrier, len(around) + len(zdevs))
-    copies[0].start()
-    copies[1].start()
-    for c in order[2:]:
+    for c in order:
         look(c)
     for l in range(2):
         for side in range(2):
@@ -128,13 +124,14 @@
             for a in range(2):
                 x, y = (X - 2) * sx + a, (Y - 2) * sy
                 faces[pl.ds(edges + 8 * (2 * sx + sy) + 2 * a, 2)] = eps[pl.ds(x * Y + y, 2)]
+    pl.semaphore_wait(barrier, len(around) + len(zdevs))
+    for dev in xdevs:
+        pl.semaphore_signal(entered, inc=1, device_id=dev, device_id_type=MESH)
+    for k in range(4):
+        copies[k].start()
     for c in order:
         for s in range(zpeers):
             mains[c, s].start()
-    for k in range(4, 8):
-        copies[k].start()
-    for k in (2, 3):
-        copies[k].start()
 
     def zfilter(e, low, high):
         lane = lax.broadcasted_iota(jnp.int32, e.shape, 1)
@@ -149,7 +146,13 @@
         low = ref[0, part]
         return low, (low if zpeers == 1 else ref[1, part])
 
-    for c in order:
+    def arrive(ks):
+        for k in ks:
+            copies[k].wait_recv()
+            for s in range(zpeers):
+                forwards[k, s].start()
+
+    for n, c in enumerate(order):
         for s in range(zpeers):
             mains[c, s].wait_recv()
 
@@ -161,6 +164,14 @@
             return carry
 
         lax.fori_loop(0, rows // Y, plane, 0)
+        if n == 0:
+            pl.semaphore_wait(entered, len(xdevs))
+            for k in range(4, 8):
+                copies[k].start()
+        elif n == 2:
+            arrive((2, 3))
+        elif n == 3:
+            arrive((0, 1))
 
     def yrows(ref, p, j, shift):
         return ref[p, PAD + 16 * j + shift:PAD + 16 * j + shift + 16]
@@ -202,12 +213,6 @@
                 return carry
 
             lax.fori_loop(0, count // unroll, block, carry)
-
-    def arrive(ks):
-        for k in ks:
-            copies[k].wait_recv()
-            for s in range(zpeers):
-                forwards[k, s].start()
 
     def halo_filter(k):
         for s in range(zpeers):
@@ -233,18 +238,21 @@
     pairs = Y // 16
     unroll = 4
     inside = range(1, pairs - 1)
-    for n, j in enumerate(inside):
+    for j in inside:
         outputs(j, 2, X - 4, unroll)
-        if n == 0:
-            arrive((2, 3))
-    arrive((0, 1, 4, 5, 6, 7))
+    arrive(range(4, 8))
     halo_filter(2)
     halo_filter(3)
     outputs(0, 2, X - 4, unroll)
     outputs(pairs - 1, 2, X - 4, unroll)
-    for k in (0, 1, 4, 5, 6, 7):
+    halo_filter(0)
+    halo_filter(1)
+    for j in inside:
+        outputs(j, 0, 2, 2)
+        outputs(j, X - 2, 2, 2)
+    for k in range(4, 8):
         halo_filter(k)
-    for j in range(pairs):
+    for j in (0, pairs - 1):
         outputs(j, 0, 2, 2)
         outputs(j, X - 2, 2, 2)
     for copy in list(copies.values()) + list(mains.values()) + list(forwards.values()):
@@ -288,6 +296,7 @@
                 dma((zpeers, CHUNKS)), dma((zpeers, CHUNKS)),
                 dma((8,)), dma((8,)),
                 dma((zpeers, 8)), dma((zpeers, 8)),
+                pltpu.SemaphoreType.REGULAR,
             ],
             compiler_params=pltpu.CompilerParams(
                 collective_id=0, has_side_effects=True, vmem_limit_bytes=24 * 2**20

time: 17.9 us -> 16.4 us (0.916)
  Pallas kernels: 17.7 us -> 16.3 us
    pallas_call x1, Pallas kernels: 16 us -> 14.6 us  [local(): pl.pallas_call(functools.partial(kernel, nx, ny, nz, X, Y), out_shape=plt...]
where the time goes in v3:
time: 16.4 us; the launch traced here: 16.3 us
  Pallas kernels  16.3 us (99%)
    pallas_call x1, Pallas kernels, local(): pl.pallas_call(functools.partial(kernel, nx, ny, nz, X, Y), out_shape=plt...  14.6 us
    pallas_call x1, Pallas kernels, local(): pl.pallas_call(write_out, out_shape=jax.ShapeDtypeStruct((6, X, Y, Z), jn...  1.71 us

profile of v3, /device:TPU:0, one launch (start us, length us, event | category | flops | bytes accessed | tf_op | source)
XLA Modules:
  0.0 16.3 jit_solution(5349329763682457916)
XLA Ops:
  0.0 14.6 %shard_map.37.result = bf16[6,32,64,128]{3,2,1,0:T(8,128)(2,1)S(1)} custom-call(s32[2048,128]{1,0:T(8,128)} %bitcast.2, f32[8]{0:T(128)} %table_hbm.1, bf16[2048,128]{1,0:T(8,128)(2,1)} %bitcast.3), custom_call_target="tpu_custom_call" | custom-call | tf_op jit(solution)/shard_map/pallas_call | solution.py:280
  14.6 1.7 %shard_map.38 = bf16[6,32,64,128]{3,2,1,0:T(8,128)(2,1)} custom-call(bf16[6,32,64,128]{3,2,1,0:T(8,128)(2,1)S(1)} %shard_map.37.result), custom_call_target="tpu_custom_call" | custom-call | tf_op jit(solution)/shard_map/pallas_call | solution.py:306

commit v4 on v3

--- a/solution.py
+++ b/solution.py
@@ -17,8 +17,55 @@
     return guess * (2.0 - x * guess)
 
 
-def kernel(nx, ny, nz, X, Y, mat_hbm, table_hbm, grad_hbm, out, mat, table, grad, eps, peer, halo, halo_peer, faces,
-           zs, zd, zi, in_sem, table_sem, main_send, main_recv, face_send, face_recv, fwd_send, fwd_recv, entered):
+def yrows(ref, p, j, shift):
+    return ref[p, PAD + 16 * j + shift:PAD + 16 * j + shift + 16]
+
+
+def lead(fields, p, j):
+    zs = fields[0]
+    a, b = yrows(zs, p, j, -1), yrows(zs, p, j, 1)
+    return yrows(zs, p, j, 0) + (a + b)
+
+
+def rest(fields, p, j):
+    zs, zd, zi = fields
+    b = (yrows(zs, p, j, 1) - yrows(zs, p, j, -1)) + (yrows(zs, p, j, 2) - yrows(zs, p, j, -2))
+    return b, sum(yrows(zd, p, j, k) for k in (-1, 0, 1)), sum(yrows(zi, p, j, k) for k in (-1, 0, 1))
+
+
+def outputs(fields, put, j, start, count, unroll):
+    def step(x, carry):
+        (a0, a1, a2, a3), r0, r1 = carry
+        a4 = lead(fields, x + 4, j)
+        r2 = rest(fields, x + 3, j)
+        total = a2 + (a1 + a3)
+        gx = (a3 - a1) + (a4 - a0)
+        gy, gz, inv = (u + v + w for u, v, w in zip(r0, r1, r2))
+        den = gx * gx + gy * gy + gz * gz + 291.6
+        q = inverse(total * den)
+        recip = (den * q) * 27.0
+        k = (inv * (1.0 / 27.0) - recip) * (total * q)
+        kx, ky, kz = gx * k, gy * k, gz * k
+        result = (gx * kx + recip, gy * ky + recip, gz * kz + recip, gx * ky, gx * kz, gy * kz)
+        for n, value in enumerate(result):
+            put(n, x, j, value)
+        return (a1, a2, a3, a4), r1, r2
+
+    carry = (tuple(lead(fields, start + k, j) for k in range(4)), rest(fields, start + 1, j), rest(fields, start + 2, j))
+    if count == unroll:
+        for k in range(count):
+            carry = step(start + k, carry)
+    else:
+        def block(i, carry):
+            for k in range(unroll):
+                carry = step(start + i * unroll + k, carry)
+            return carry
+
+        lax.fori_loop(0, count // unroll, block, carry)
+
+
+def kernel(nx, ny, nz, X, Y, mat_hbm, table_hbm, grad_hbm, out, zs, zd, zi, mat, table, grad, eps, peer,
+           halo, halo_peer, faces, in_sem, table_sem, main_send, main_recv, face_send, face_recv, fwd_send, fwd_recv, entered):
     Z = mat.shape[-1]
     zpeers = 1 if nz == 2 else 2
     xs, ys = 2 * Y, 2 * X
@@ -173,47 +220,6 @@
         elif n == 3:
             arrive((0, 1))
 
-    def yrows(ref, p, j, shift):
-        return ref[p, PAD + 16 * j + shift:PAD + 16 * j + shift + 16]
-
-    def lead(p, j):
-        a, b = yrows(zs, p, j, -1), yrows(zs, p, j, 1)
-        return yrows(zs, p, j, 0) + (a + b)
-
-    def rest(p, j):
-        b = (yrows(zs, p, j, 1) - yrows(zs, p, j, -1)) + (yrows(zs, p, j, 2) - yrows(zs, p, j, -2))
-        return b, sum(yrows(zd, p, j, k) for k in (-1, 0, 1)), sum(yrows(zi, p, j, k) for k in (-1, 0, 1))
-
-    def outputs(j, start, count, unroll):
-        def step(x, carry):
-            (a0, a1, a2, a3), r0, r1 = carry
-            a4 = lead(x + 4, j)
-            r2 = rest(x + 3, j)
-            total = a2 + (a1 + a3)
-            gx = (a3 - a1) + (a4 - a0)
-            gy, gz, inv = (u + v + w for u, v, w in zip(r0, r1, r2))
-            den = gx * gx + gy * gy + gz * gz + 291.6
-            q = inverse(total * den)
-            recip = (den * q) * 27.0
-            k = (inv * (1.0 / 27.0) - recip) * (total * q)
-            kx, ky, kz = gx * k, gy * k, gz * k
-            result = (gx * kx + recip, gy * ky + recip, gz * kz + recip, gx * ky, gx * kz, gy * kz)
-            for n, value in enumerate(result):
-                out[n, x, 16 * j:16 * j + 16] = value.astype(out.dtype)
-            return (a1, a2, a3, a4), r1, r2
-
-        carry = (tuple(lead(start + k, j) for k in range(4)), rest(start + 1, j), rest(start + 2, j))
-        if count == unroll:
-            for k in range(count):
-                carry = step(start + k, carry)
-        else:
-            def block(i, carry):
-                for k in range(unroll):
-                    carry = step(start + i * unroll + k, carry)
-                return carry
-
-            lax.fori_loop(0, count // unroll, block, carry)
-
     def halo_filter(k):
         for s in range(zpeers):
             forwards[k, s].wait_recv()
@@ -238,31 +244,47 @@
     pairs = Y // 16
     unroll = 4
     inside = range(1, pairs - 1)
+    fields = (zs, zd, zi)
+
+    def put(n, x, j, value):
+        out[n, x, 16 * j:16 * j + 16] = value.astype(out.dtype)
+
     for j in inside:
-        outputs(j, 2, X - 4, unroll)
-    arrive(range(4, 8))
+        outputs(fields, put, j, 2, X - 4, unroll)
     halo_filter(2)
     halo_filter(3)
-    outputs(0, 2, X - 4, unroll)
-    outputs(pairs - 1, 2, X - 4, unroll)
-    halo_filter(0)
-    halo_filter(1)
-    for j in inside:
-        outputs(j, 0, 2, 2)
-        outputs(j, X - 2, 2, 2)
-    for k in range(4, 8):
+    outputs(fields, put, 0, 2, X - 4, unroll)
+    arrive(range(4, 8))
+    outputs(fields, put, pairs - 1, 2, X - 4, unroll)
+    for k in (0, 1, 4, 5, 6, 7):
         halo_filter(k)
-    for j in (0, pairs - 1):
-        outputs(j, 0, 2, 2)
-        outputs(j, X - 2, 2, 2)
     for copy in list(copies.values()) + list(mains.values()) + list(forwards.values()):
         copy.wait_send()
 
 
-def write_out(result, out, sem):
-    copies = [pltpu.make_async_copy(result.at[n], out.at[n], sem.at[n]) for n in range(out.shape[0])]
+def write_out(result, zs, zd, zi, out, ends, sem, end_sem):
+    _, X, Y, _ = out.shape
+    inner = pl.ds(2, X - 4)
+    copies = [
+        pltpu.make_async_copy(result.at[n, inner], out.at[n, inner], sem.at[n]) for n in range(out.shape[0])
+    ]
     for copy in copies:
         copy.start()
+    for side in range(2):
+        start = side * (X - 2)
+
+        def put(n, x, j, value):
+            ends[side, n, x - start, 16 * j:16 * j + 16] = value.astype(out.dtype)
+
+        for j in range(Y // 16):
+            outputs((zs, zd, zi), put, j, start, 2, 2)
+        tail = [
+            pltpu.make_async_copy(ends.at[side, n], out.at[n, pl.ds(start, 2)], end_sem.at[side, n])
+            for n in range(out.shape[0])
+        ]
+        for copy in tail:
+            copy.start()
+        copies += tail
     for copy in copies:
         copy.wait()
 
@@ -276,12 +298,13 @@
         halo_rows = 4 * Y + 4 * X + 32
         any_space = pl.BlockSpec(memory_space=pl.ANY)
         dma = pltpu.SemaphoreType.DMA
+        vmem = pl.BlockSpec(memory_space=pltpu.VMEM)
         field = pltpu.VMEM((X + 4, Y + 2 * PAD, Z), jnp.float32)
         result = pl.pallas_call(
             functools.partial(kernel, nx, ny, nz, X, Y),
-            out_shape=pltpu.VMEM((6, X, Y, Z), jnp.bfloat16),
+            out_shape=(pltpu.VMEM((6, X, Y, Z), jnp.bfloat16), field, field, field),
             in_specs=[pl.BlockSpec(memory_space=pltpu.HBM)] * 3,
-            out_specs=pl.BlockSpec(memory_space=pltpu.VMEM),
+            out_specs=(vmem,) * 4,
             scratch_shapes=[
                 pltpu.VMEM((X * Y, Z), jnp.int32),
                 pltpu.SMEM(eps_table.shape, jnp.float32),
@@ -291,7 +314,6 @@
                 pltpu.VMEM((halo_rows, Z), jnp.float32),
                 pltpu.VMEM((zpeers, halo_rows, Z), jnp.float32),
                 pltpu.VMEM((4 * X + 32, Z), jnp.float32),
-                field, field, field,
                 dma((2, CHUNKS)), dma(()),
                 dma((zpeers, CHUNKS)), dma((zpeers, CHUNKS)),
                 dma((8,)), dma((8,)),
@@ -306,11 +328,11 @@
         return pl.pallas_call(
             write_out,
             out_shape=jax.ShapeDtypeStruct((6, X, Y, Z), jnp.bfloat16),
-            in_specs=[pl.BlockSpec(memory_space=pltpu.VMEM)],
+            in_specs=[vmem] * 4,
             out_specs=any_space,
-            scratch_shapes=[dma((6,))],
+            scratch_shapes=[pltpu.VMEM((2, 6, 2, Y, Z), jnp.bfloat16), dma((6,)), dma((2, 6))],
             compiler_params=pltpu.CompilerParams(vmem_limit_bytes=24 * 2**20),
-        )(result)
+        )(*result)
 
     return jax.shard_map(
         local,

time: 16.4 us -> 15.6 us (0.951)
  Pallas kernels: 16.3 us -> 15.5 us
    pallas_call x1, Pallas kernels: 14.6 us -> 13.7 us  [local(): pl.pallas_call(functools.partial(kernel, nx, ny, nz, X, Y), out_shape=(pl...]
where the time goes in v4:
time: 15.6 us; the launch traced here: 15.5 us
  Pallas kernels  15.5 us (99%)
    pallas_call x1, Pallas kernels, local(): pl.pallas_call(functools.partial(kernel, nx, ny, nz, X, Y), out_shape=(pl...  13.7 us
    pallas_call x1, Pallas kernels, local(): pl.pallas_call(write_out, out_shape=jax.ShapeDtypeStruct((6, X, Y, Z), jn...  1.8 us

profile of v4, /device:TPU:0, one launch (start us, length us, event | category | flops | bytes accessed | tf_op | source)
XLA Modules:
  0.0 15.5 jit_solution(7570505176604553729)
XLA Ops:
  0.0 13.7 %shard_map.37 = (bf16[6,32,64,128]{3,2,1,0:T(8,128)(2,1)S(1)}, f32[36,80,128]{2,1,0:T(8,128)S(1)}, f32[36,80,128]{2,1,0:T(8,128)S(1)}, f32[36,80,128]{2,1,0:T(8,128)S(1)}) custom-call(s32[2048,128]{1,0:T(8,128)} %bitcast.2, f32[8]{0:T(128)} %table_hbm.1, bf16[2048,128]{1,0:T(8,128)(2,1)} %bitcast.3), custom_call_target="tpu_custom_call" | custom-call | tf_op jit(solution)/shard_map/pallas_call | solution.py:303
  13.7 1.8 %shard_map.38 = bf16[6,32,64,128]{3,2,1,0:T(8,128)(2,1)} custom-call(bf16[6,32,64,128]{3,2,1,0:T(8,128)(2,1)S(1)} %get-tuple-element.9.result, f32[36,80,128]{2,1,0:T(8,128)S(1)} %get-tuple-element.10.zs, f32[36,80,128]{2,1,0:T(8,128)S(1)} %get-tuple-element.11.zd, f32[36,80,128]{2,1,0:T(8,128)S(1)} %get-tuple-element.12.zi), custom_call_target="tpu_custom_call" | custom-call | tf_op jit(solution)/shard_map/pallas_call | solution.py:328
